TPU v7x, 128 devices: a whole 4x4x4 slice. The times are simulated.
128 devices in a mesh: ka: 16 (over x_hi, z, core), band: 8 (over x_lo, y).
Axes of the slice: x: 4 (x_hi: 2, x_lo: 2; x = x_hi * 2 + x_lo), y: 4, z: 4, core: 2. Of those that a mesh axis runs over, the one named last changes fastest.
Arguments:
- occ_rows: bfloat16 [16, 2048, 128], P('ka', 'band'), may hold values from -0.5 to 0.5
- vir_rows: bfloat16 [16, 2048, 896], P('ka', 'band'), may hold values from -0.1875 to 0.1875
- trial_vectors: float32 [16, 2, 128, 896], P('ka', None, None, 'band'), may hold values from -6 to 6
- occ_energy: float32 [16, 128], P('ka'), may hold values from -1.2 to -0.3
- vir_energy: float32 [16, 896], P('ka', 'band'), may hold values from 0.1 to 1.5
- coulomb: bfloat16 [2048, 2048], P('band'), may hold values from -0.0625 to 0.0625
- exch_kernel: bfloat16 [16, 2048, 2048], P(None, 'band'), as said below
- minus_table: int32 [16, 16], replicated, may hold values from 0 to 15, as said below
Outputs:
- sigma_vectors: float32 [16, 2, 128, 896], P('ka', None, None, 'band')
Inputs may be any that keep to these rules, and one draw needn't show every extreme that they name: minus_table[k, q] is the k-point k - q on a group of 16 k-points: every row and every column holds each index once, and one q gives minus_table[k, q] == k for every k. Each exch_kernel[q] is symmetric.
All inputs are finite; a program needn't handle non-finite values.
Results may differ from a plain program's by a relative error of at most 0.0051.
Values may be sent and summed in bfloat16 or wider, within the bound.
A program may use at most 128 MiB of HBM per device.

v0:
```python
import jax
import jax.numpy as jnp
from jax import lax
from jax.sharding import PartitionSpec as P


def sent_to_all(array, axis):
    copies = jnp.broadcast_to(array, (lax.axis_size(axis), *array.shape))
    return lax.all_to_all(copies, axis, split_axis=0, concat_axis=0, tiled=True)


def taken_together(array, axis):
    return sent_to_all(array, axis).sum(axis=0)


def in_order(pieces, dim):
    pieces = jnp.moveaxis(pieces, 0, dim)
    dims = pieces.shape
    return pieces.reshape(*dims[:dim], dims[dim] * dims[dim + 1], *dims[dim + 2 :])


def gather_directly(array, axis, dim):
    pieces = sent_to_all(array, axis)
    return in_order(pieces, dim)


def split_up(array, dim, size):
    before, after = (array.shape[:dim], array.shape[dim + 1 :])
    return jnp.moveaxis(array.reshape(*before, size, -1, *after), dim, 0)


def summed_on_arrival(array, axis, dim):
    size = lax.axis_size(axis)
    pieces = lax.all_to_all(split_up(array, dim, size), axis, 0, 0, tiled=True)
    return jnp.sum(pieces, axis=0)


def per_device(
    occ_rows, vir_rows, trial_vectors, occ_energy, vir_energy, coulomb, exch_kernel, minus_table
):
    vectors = trial_vectors.shape[1]
    own_rows = occ_rows.shape[1]
    kpoints = lax.axis_size("ka")
    self_point = lax.axis_index("ka")
    trial_half = trial_vectors[0].astype(jnp.bfloat16)
    trial_full, vir_full = (
        lax.all_gather(trial_half, "band", axis=2, tiled=True),
        lax.all_gather(vir_rows[0], "band", axis=0, tiled=True),
    )
    auxiliary = vir_full.shape[0]
    occ_own = occ_rows[0]
    vir_own = vir_rows[0]
    mixed_rows = jnp.einsum(
        "ri,via->vra", occ_own, trial_full, preferred_element_type=jnp.float32
    ).astype(jnp.bfloat16)
    pair_block = jnp.einsum(
        "vra,na->vrn", mixed_rows, vir_full, preferred_element_type=jnp.float32
    ).astype(jnp.bfloat16)
    density_own = jnp.sum(
        mixed_rows.astype(jnp.float32) * vir_own.astype(jnp.float32)[None], axis=2
    )
    density_sum = taken_together(density_own, "ka")
    density_half = gather_directly(density_sum.astype(jnp.bfloat16), "band", 1)
    potential = jnp.einsum("vn,rn->vr", density_half, coulomb, preferred_element_type=jnp.float32)
    piece_width = auxiliary // kpoints
    kernel_cols = lax.dynamic_slice_in_dim(exch_kernel, self_point * piece_width, piece_width, 2)
    split_pairs = pair_block.reshape(vectors, own_rows, kpoints, piece_width)
    moved_pairs = jnp.take(
        lax.all_to_all(split_pairs, "ka", split_axis=2, concat_axis=2, tiled=True),
        minus_table,
        axis=2,
    )
    summed = jnp.einsum(
        "vrkqc,qrc->vrkc", moved_pairs, kernel_cols, preferred_element_type=jnp.float32
    )
    screened = lax.all_to_all(
        summed.astype(jnp.bfloat16), "ka", split_axis=2, concat_axis=2, tiled=True
    )
    screened = screened.reshape(vectors, own_rows, auxiliary)
    product = jnp.einsum("vrn,na->vra", screened, vir_full, preferred_element_type=jnp.float32)
    weights = (2.0 * potential[:, :, None] * vir_own.astype(jnp.float32)[None] - product).astype(
        jnp.bfloat16
    )
    partial_sums = jnp.einsum("ri,vra->via", occ_own, weights, preferred_element_type=jnp.float32)
    coupled = summed_on_arrival(partial_sums, "band", 2)
    energy_gaps = vir_energy[0][None, :] - occ_energy[0][:, None]
    return (energy_gaps[None] * trial_vectors[0] + coupled)[None]


def solution(mesh):
    in_specs = (
        P("ka", "band", None),
        P("ka", "band", None),
        P("ka", None, None, "band"),
        P("ka", None),
        P("ka", "band"),
        P("band", None),
        P(None, "band", None),
        P(),
    )
    out_specs = P("ka", None, None, "band")
    return jax.shard_map(
        per_device, mesh=mesh, in_specs=in_specs, out_specs=out_specs, check_vma=False
    )
```

profile of v0, /device:TPU:96, one launch (start us, length us, event | category | flops | bytes accessed | tf_op | source)
XLA Modules:
  0.0 215.4 jit_solution(1257399889311923718)
XLA Ops:
  6.5 0.7 all-gather.4.cloned.1.call-update
  7.3 1.1 bitcast_convert_fusion.1
  8.3 0.3 copy.30
  8.7 31.1 %all-gather = bf16[1,2,128,896]{2,3,1,0:T(8,128)(2,1)S(1)} all-gather(bf16[1,2,128,112]{2,3,1,0:T(8,128)(2,1)S(1)} %convert_element_type.33), channel_id=2, replica_groups=mesh['ka'=16,'band'=8] {'band'}, dimensions={3}, use_global_device_ids=true | all-gather | bytes 516096 | tf_op jit(solution)/shard_map/all_gather | solution.py:47
  39.7 0.4 multiply_reduce_fusion.1
  40.2 0.6 broadcast_in_dim.23
  40.8 6.5 %all-to-all-start = ((f32[16,2,256]{2,1,0:T(2,128)}), f32[16,2,256]{2,1,0:T(2,128)S(1)}, u32[]{:S(2)}, u32[]{:S(2)}) async-start(f32[16,2,256]{2,1,0:T(2,128)} %broadcast_in_dim.23), calls=%async_computation | async-start | bytes 65536 | tf_op jit(solution)/shard_map/all_to_all | solution.py:9
  47.3 13.7 %all-gather.4.cloned.1.call-done = bf16[1,2048,896]{2,1,0:T(8,128)(2,1)} async-done(((bf16[1,256,896]{2,1,0:T(8,128)(2,1)}), bf16[1,2048,896]{2,1,0:T(8,128)(2,1)}) %all-gather.4.cloned.1.call-update) | async-done | bytes 3670032 | tf_op jit(solution)/shard_map/all_gather | solution.py:48
  61.0 4.4 %fusion.7 = bf16[2,32,16,8,128]{4,3,2,1,0:T(8,128)(2,1)S(1)} fusion(bf16[2,256,896]{1,2,0:T(8,128)(2,1)S(1)} %get-tuple-element.6, bf16[1,2048,896]{2,1,0:T(8,128)(2,1)} %all-gather.4.cloned.1.call-done), kind=kOutput, calls=%fused_computation.11 | convolution fusion | flops 1880096768 | bytes 6684672 | tf_op jit(solution)/shard_map/vra,na->vrn/dot_general | solution.py:56
  65.5 1.9 copy.55
  67.4 6.8 %all-to-all-start.2 = ((bf16[2,256,16,128]{3,1,0,2:T(8,128)(2,1)}), bf16[2,256,16,128]{3,1,0,2:T(8,128)(2,1)S(1)}, u32[]{:S(2)}, u32[]{:S(2)}) async-start(bf16[2,256,16,128]{3,1,0,2:T(8,128)(2,1)} %bitcast.66), calls=%async_computation.2 | async-start | bytes 4194304 | tf_op jit(solution)/shard_map/all_to_all | solution.py:69
  74.2 0.1 reshape.57
  74.3 2.7 %bitcast_convert_fusion = f32[256,128,16]{1,0,2:T(8,128)} fusion(bf16[16,256,2048]{2,1,0:T(8,128)(2,1)} %param.14, s32[]{:T(128)S(6)} %select_n.12), kind=kLoop, calls=%fused_computation.16 | loop fusion | flops 524288 | bytes 3145732
  77.0 26.1 %all-to-all-done.2 = bf16[2,256,16,128]{3,1,0,2:T(8,128)(2,1)S(1)} async-done(((bf16[2,256,16,128]{3,1,0,2:T(8,128)(2,1)}), bf16[2,256,16,128]{3,1,0,2:T(8,128)(2,1)S(1)}, u32[]{:S(2)}, u32[]{:S(2)}) %all-to-all-start.2) | async-done | bytes 2097184 | tf_op jit(solution)/shard_map/all_to_all | solution.py:69
  103.1 0.6 broadcast_in_dim.24
  103.7 0.7 copy-done.1
  104.4 4.2 %all-to-all-start.1 = ((bf16[8,2,256]{2,1,0:T(2,128)(2,1)}), bf16[8,2,256]{2,1,0:T(2,128)(2,1)S(1)}, u32[]{:S(2)}, u32[]{:S(2)}) async-start(bf16[8,2,256]{2,1,0:T(2,128)(2,1)} %broadcast_in_dim.24), calls=%async_computation.1 | async-start | bytes 16384 | tf_op jit(solution)/shard_map/all_to_all | solution.py:9
  108.6 1.7 copy.34
  110.3 13.9 %gather_fusion = bf16[256,2,256,128]{3,2,1,0:T(8,128)(2,1)} fusion(bf16[2,256,16,128]{3,1,2,0:T(8,128)(2,1)S(1)} %copy.34, s32[1024]{0:T(1024)S(1)} %pad_clamp_fusion), kind=kCustom, calls=%fused_computation | custom fusion | bytes 67109888 | tf_op jit(solution)/shard_map/jit(_take)/gather | solution.py:68
  124.2 17.9 %multiply_reduce_fusion = bf16[256,128,2,16]{1,0,2,3:T(8,128)(2,1)S(1)} fusion(f32[256,128,16]{1,0,2:T(8,128)} %bitcast_convert_fusion, bf16[16,16,2,256,128]{4,3,2,1,0:T(8,128)(2,1)} %bitcast.65, pred[16,16]{1,0:T(8,128)(4,1)S(1)} %compare_and_fusion), kind=kLoop, calls=%fused_computation.1 | loop fusion | flops 66060288 | bytes 37748992
  142.1 2.6 %copy.47 = bf16[256,128,2,16]{0,1,2,3:T(8,128)(2,1)} copy(bf16[256,128,2,16]{1,0,2,3:T(8,128)(2,1)S(1)} %multiply_reduce_fusion) | data formatting | bytes 4194304 | tf_op jit(solution)/shard_map/vrkqc,qrc->vrkc/dot_general | solution.py:73
  144.7 5.5 %all-to-all-start.3 = ((bf16[2,256,16,128]{1,3,0,2:T(8,128)(2,1)}), bf16[2,256,16,128]{1,3,0,2:T(8,128)(2,1)S(1)}, u32[]{:S(2)}, u32[]{:S(2)}) async-start(bf16[2,256,16,128]{1,3,0,2:T(8,128)(2,1)} %bitcast.67), calls=%async_computation.3 | async-start | bytes 4194304 | tf_op jit(solution)/shard_map/all_to_all | solution.py:76
  150.3 0.4 convolution_multiply_fusion
  150.6 28.5 %all-to-all-done.3 = bf16[2,256,16,128]{1,3,0,2:T(8,128)(2,1)S(1)} async-done(((bf16[2,256,16,128]{1,3,0,2:T(8,128)(2,1)}), bf16[2,256,16,128]{1,3,0,2:T(8,128)(2,1)S(1)}, u32[]{:S(2)}, u32[]{:S(2)}) %all-to-all-start.3) | async-done | bytes 2097184 | tf_op jit(solution)/shard_map/all_to_all | solution.py:76
  179.2 1.5 copy.35
  180.7 5.6 %fusion.14 = f32[2,896,128]{2,1,0:T(8,128)S(1)} fusion(bf16[2,256,2048]{1,2,0:T(8,128)(2,1)} %bitcast.68, bf16[1,2048,896]{2,1,0:T(8,128)(2,1)} %all-gather.4.cloned.1.call-done, f32[2,256]{1,0:T(2,128)S(1)} %convolution_multiply_fusion, f32[256,896]{0,1:T(8,128)} %copy-done.2, bf16[1,256,128]{2,1,0:T(8,128)(2,1)S(1)} %copy-done.4), kind=kOutput, calls=%fused_computation.14 | convolution fusion | flops 1997864960 | bytes 7669760 | tf_op jit(solution)/shard_map/ri,vra->via/dot_general | solution.py:84
  186.2 0.0 copy-start.7
  186.3 1.0 copy.56
  187.2 6.6 %all-to-all-start.4 = ((f32[8,2,128,112]{2,3,1,0:T(8,128)}), f32[8,2,128,112]{2,3,1,0:T(8,128)S(1)}, u32[]{:S(2)}, u32[]{:S(2)}) async-start(f32[8,2,128,112]{2,3,1,0:T(8,128)} %bitcast.64), calls=%async_computation.4 | async-start | bytes 1835008 | tf_op jit(solution)/shard_map/all_to_all | solution.py:34
  193.9 0.1 broadcast_subtract_fusion
  194.0 13.9 %all-to-all-done.4 = f32[8,2,128,112]{2,3,1,0:T(8,128)S(1)} async-done(((f32[8,2,128,112]{2,3,1,0:T(8,128)}), f32[8,2,128,112]{2,3,1,0:T(8,128)S(1)}, u32[]{:S(2)}, u32[]{:S(2)}) %all-to-all-start.4) | async-done | bytes 917536 | tf_op jit(solution)/shard_map/all_to_all | solution.py:34
  207.9 0.7 bitcast_add_fusion
  (23 shorter events, 0.1 us)
Async XLA Ops:
  6.5 143.7 %copy-start = (bf16[256,2048]{1,0:T(8,128)(2,1)S(1)}, bf16[256,2048]{1,0:T(8,128)(2,1)}, u32[]{:S(2)}) copy-start(bf16[256,2048]{1,0:T(8,128)(2,1)} %param.13) | copy-start | bytes 3145732
  6.5 2.1 copy-start.3
  6.5 33.2 %copy-start.4 = (bf16[1,256,128]{2,1,0:T(8,128)(2,1)S(1)}, bf16[1,256,128]{2,1,0:T(8,128)(2,1)}, u32[]{:S(2)}) copy-start(bf16[1,256,128]{2,1,0:T(8,128)(2,1)} %param.8) | copy-start | bytes 196612
  6.5 54.5 %all-gather.4.cloned.1.call-start = ((), (), s32[]{:S(2)}) async-start(), calls=%async_computation.5 | async-start | bytes 4128768 | tf_op jit(solution)/shard_map/all_gather | solution.py:48
  8.7 56.8 %copy-start.2 = (f32[256,896]{0,1:T(8,128)}, f32[256,896]{0,1:T(8,128)S(1)}, u32[]{:S(2)}) copy-start(f32[256,896]{0,1:T(8,128)S(1)} %copy.30) | copy-start | bytes 2752516
  40.8 26.6 %all-to-all-start = ((f32[16,2,256]{2,1,0:T(2,128)}), f32[16,2,256]{2,1,0:T(2,128)S(1)}, u32[]{:S(2)}, u32[]{:S(2)}) async-start(f32[16,2,256]{2,1,0:T(2,128)} %broadcast_in_dim.23), calls=%async_computation | async-start | bytes 65536 | tf_op jit(solution)/shard_map/all_to_all | solution.py:9
  67.4 6.8 %copy-start.5 = (s32[16,16]{1,0:T(8,128)S(1)}, s32[16,16]{1,0:T(8,128)}, u32[]{:S(2)}) copy-start(s32[16,16]{1,0:T(8,128)} %param.15) | copy-start | bytes 3076
  67.4 35.7 %all-to-all-start.2 = ((bf16[2,256,16,128]{3,1,0,2:T(8,128)(2,1)}), bf16[2,256,16,128]{3,1,0,2:T(8,128)(2,1)S(1)}, u32[]{:S(2)}, u32[]{:S(2)}) async-start(bf16[2,256,16,128]{3,1,0,2:T(8,128)(2,1)} %bitcast.66), calls=%async_computation.2 | async-start | bytes 4194304 | tf_op jit(solution)/shard_map/all_to_all | solution.py:69
  103.1 1.3 copy-start.1
  104.4 40.3 %all-to-all-start.1 = ((bf16[8,2,256]{2,1,0:T(2,128)(2,1)}), bf16[8,2,256]{2,1,0:T(2,128)(2,1)S(1)}, u32[]{:S(2)}, u32[]{:S(2)}) async-start(bf16[8,2,256]{2,1,0:T(2,128)(2,1)} %broadcast_in_dim.24), calls=%async_computation.1 | async-start | bytes 16384 | tf_op jit(solution)/shard_map/all_to_all | solution.py:9
  144.7 34.5 %all-to-all-start.3 = ((bf16[2,256,16,128]{1,3,0,2:T(8,128)(2,1)}), bf16[2,256,16,128]{1,3,0,2:T(8,128)(2,1)S(1)}, u32[]{:S(2)}, u32[]{:S(2)}) async-start(bf16[2,256,16,128]{1,3,0,2:T(8,128)(2,1)} %bitcast.67), calls=%async_computation.3 | async-start | bytes 4194304 | tf_op jit(solution)/shard_map/all_to_all | solution.py:76
  186.2 7.6 %copy-start.6 = (f32[1,128]{1,0:T(1,128)S(1)}, f32[1,128]{1,0:T(1,128)}, u32[]{:S(2)}) copy-start(f32[1,128]{1,0:T(1,128)} %param.11) | copy-start | bytes 1540
  186.2 7.6 %copy-start.7 = (f32[1,112]{1,0:T(1,128)S(1)}, f32[1,112]{1,0:T(1,128)}, u32[]{:S(2)}) copy-start(f32[1,112]{1,0:T(1,128)} %param.12) | copy-start | bytes 1348
  187.2 20.6 %all-to-all-start.4 = ((f32[8,2,128,112]{2,3,1,0:T(8,128)}), f32[8,2,128,112]{2,3,1,0:T(8,128)S(1)}, u32[]{:S(2)}, u32[]{:S(2)}) async-start(f32[8,2,128,112]{2,3,1,0:T(8,128)} %bitcast.64), calls=%async_computation.4 | async-start | bytes 1835008 | tf_op jit(solution)/shard_map/all_to_all | solution.py:34
Sparse Core Ops, SparseCore 0:
  9.0 52.0 all-gather.3
where the time goes:
time: 216 us; the launch traced here: 215 us
  waiting for transfers between devices  82.9 us (38%)
  blocking collectives  31.1 us (14%)
  starting transfers between devices  29.6 us (14%)
  local copies, waits for them, and re-layouts  25 us (12%)
  other arithmetic  22.5 us (10%)
  between operations  13.5 us (6%)
  matrix products  10.8 us (5%)
    all_gather x1, blocking collectives, per_device(): lax.all_gather(trial_half, 'band', axis=2, tiled=True)  31.1 us
    all_to_all x1, waiting for transfers between devices, per_device(): lax.all_to_all(summed.astype(jnp.bfloat16), 'ka', split_axis=2, concat_ax...  28.5 us
    all_to_all x1, waiting for transfers between devices, per_device(): lax.all_to_all(split_pairs, 'ka', split_axis=2, concat_axis=2, tiled=True)  26.1 us
    unnamed x2, other arithmetic  20.6 us
    gather x1, local copies, waits for them, and re-layouts, per_device(): jnp.take(lax.all_to_all(split_pairs, 'ka', split_axis=2, concat_axis=2, t...  13.9 us
    all_to_all x1, waiting for transfers between devices, summed_on_arrival(): pieces = lax.all_to_all(split_up(array, dim, size), axis, 0, 0, tiled=True)  13.9 us
    all_gather x1, waiting for transfers between devices, per_device(): lax.all_gather(vir_rows[0], 'band', axis=0, tiled=True)  13.7 us
    all_to_all x2, starting transfers between devices, sent_to_all(): return lax.all_to_all(copies, axis, split_axis=0, concat_axis=0, tiled=True)  10.7 us
  transfers between devices with their start and end apart: 6, of which 4 were waited for; matrix products, arithmetic and copies ran while one was open for 22% of the time, Pallas kernels for 0%

commit v1 on v0

--- a/solution.py
+++ b/solution.py
@@ -2,6 +2,7 @@
 import jax.numpy as jnp
 from jax import lax
 from jax.sharding import PartitionSpec as P
+from jax.lax import all_to_all, axis_size
 
 
 def sent_to_all(array, axis):
@@ -43,9 +44,14 @@
     kpoints = lax.axis_size("ka")
     self_point = lax.axis_index("ka")
     trial_half = trial_vectors[0].astype(jnp.bfloat16)
+
+    def digits_rest(a_name, block_in):
+        block_out = all_to_all(jnp.stack(axis_size(a_name) * [block_in]), a_name, 0, 0)
+        return jnp.concatenate(block_out, axis=0)
+
     trial_full, vir_full = (
         lax.all_gather(trial_half, "band", axis=2, tiled=True),
-        lax.all_gather(vir_rows[0], "band", axis=0, tiled=True),
+        digits_rest("band", vir_rows[0]),
     )
     auxiliary = vir_full.shape[0]
     occ_own = occ_rows[0]

time: 216 us -> 233 us (1.079)
  blocking collectives: 31.1 us -> 66.2 us
  waiting for transfers between devices: 82.9 us -> 68.5 us
  between operations: 13.5 us -> 0.16 us
  starting transfers between devices: 29.6 us -> 35.9 us
  local copies, waits for them, and re-layouts: 25 us -> 28.9 us
    all_gather x1, blocking collectives: 31.1 us -> 66.2 us  [per_device(): lax.all_gather(trial_half, 'band', axis=2, tiled=True)]
    all_gather x1 -> x0, waiting for transfers between devices: 13.7 us -> none  [per_device(): lax.all_gather(vir_rows[0], 'band', axis=0, tiled=True)]
    all_to_all x0 -> x1, starting transfers between devices: none -> 5.53 us  [digits_rest(): all_to_all(jnp.stack(axis_size(a_name) * [block_in]), a_name, 0, 0)]
    another operation x0 -> x1, local copies, waits for them, and re-layouts: none -> 3.38 us  [digits_rest(): jnp.stack(axis_size(a_name) * [block_in])]
  transfers between devices with their start and end apart: 6 -> 6, of which waited for: 4 -> 3; matrix products, arithmetic and copies ran while one was open for 22% -> 20% of each run, Pallas kernels for 0% -> 0%
where the time goes in v1:
time: 233 us; the launch traced here: 232 us
  waiting for transfers between devices  68.5 us (29%)
  blocking collectives  66.2 us (28%)
  starting transfers between devices  35.9 us (15%)
  local copies, waits for them, and re-layouts  28.9 us (12%)
  other arithmetic  21.5 us (9%)
  matrix products  10.8 us (5%)
    all_gather x1, blocking collectives, per_device(): lax.all_gather(trial_half, 'band', axis=2, tiled=True)  66.2 us
    all_to_all x1, waiting for transfers between devices, per_device(): lax.all_to_all(summed.astype(jnp.bfloat16), 'ka', split_axis=2, concat_ax...  28.5 us
    all_to_all x1, waiting for transfers between devices, per_device(): lax.all_to_all(split_pairs, 'ka', split_axis=2, concat_axis=2, tiled=True)  26.1 us
    unnamed x2, other arithmetic  20.6 us
    gather x1, local copies, waits for them, and re-layouts, per_device(): jnp.take(lax.all_to_all(split_pairs, 'ka', split_axis=2, concat_axis=2, t...  13.9 us
    all_to_all x1, waiting for transfers between devices, summed_on_arrival(): pieces = lax.all_to_all(split_up(array, dim, size), axis, 0, 0, tiled=True)  13.9 us
    all_to_all x2, starting transfers between devices, sent_to_all(): return lax.all_to_all(copies, axis, split_axis=0, concat_axis=0, tiled=True)  10.4 us
    all_to_all x1, starting transfers between devices, per_device(): lax.all_to_all(split_pairs, 'ka', split_axis=2, concat_axis=2, tiled=True)  7.36 us
  transfers between devices with their start and end apart: 6, of which 3 were waited for; matrix products, arithmetic and copies ran while one was open for 20% of the time, Pallas kernels for 0%

profile of v1, /device:TPU:96, one launch (start us, length us, event | category | flops | bytes accessed | tf_op | source)
XLA Modules:
  0.0 231.9 jit_solution(280376242592551616)
XLA Ops:
  0.0 3.4 %stack.3 = bf16[8,256,896]{2,1,0:T(8,128)(2,1)} broadcast(bf16[256,896]{1,0:T(8,128)(2,1)} %bitcast.59), dimensions={1,2} | broadcast | bytes 4128768 | tf_op jit(solution)/shard_map/stack | solution.py:49
  3.4 5.5 %all-to-all-start.2 = ((bf16[8,256,896]{2,1,0:T(8,128)(2,1)}), bf16[8,256,896]{2,1,0:T(8,128)(2,1)}, u32[]{:S(2)}, u32[]{:S(2)}) async-start(bf16[8,256,896]{2,1,0:T(8,128)(2,1)} %stack.3), calls=%async_computation.2 | async-start | bytes 7340032 | tf_op jit(solution)/shard_map/all_to_all | solution.py:49
  8.9 0.1 bitcast_convert_fusion.1
  9.0 0.3 copy.30
  9.3 0.5 copy-done.4
  9.8 66.2 %all-gather = bf16[1,2,128,896]{2,3,1,0:T(8,128)(2,1)S(1)} all-gather(bf16[1,2,128,112]{2,3,1,0:T(8,128)(2,1)S(1)} %convert_element_type.33), channel_id=2, replica_groups=mesh['ka'=16,'band'=8] {'band'}, dimensions={3}, use_global_device_ids=true | all-gather | bytes 516096 | tf_op jit(solution)/shard_map/all_gather | solution.py:53
  76.1 0.4 multiply_reduce_fusion.1
  76.5 0.6 broadcast_in_dim.23
  77.1 6.7 %all-to-all-start = ((f32[16,2,256]{2,1,0:T(2,128)}), f32[16,2,256]{2,1,0:T(2,128)S(1)}, u32[]{:S(2)}, u32[]{:S(2)}) async-start(f32[16,2,256]{2,1,0:T(2,128)} %broadcast_in_dim.23), calls=%async_computation | async-start | bytes 65536 | tf_op jit(solution)/shard_map/all_to_all | solution.py:10
  83.8 4.4 %fusion = bf16[2,32,16,8,128]{4,3,2,1,0:T(8,128)(2,1)S(1)} fusion(bf16[2,256,896]{1,2,0:T(8,128)(2,1)S(1)} %get-tuple-element.6, bf16[2048,896,1]{1,0,2:T(8,128)(2,1)} %bitcast.12), kind=kOutput, calls=%fused_computation.7 | convolution fusion | flops 1880096768 | bytes 6684672 | tf_op jit(solution)/shard_map/vra,na->vrn/dot_general | solution.py:62
  88.2 1.9 copy.55
  90.2 7.4 %all-to-all-start.3 = ((bf16[2,256,16,128]{3,1,0,2:T(8,128)(2,1)}), bf16[2,256,16,128]{3,1,0,2:T(8,128)(2,1)S(1)}, u32[]{:S(2)}, u32[]{:S(2)}) async-start(bf16[2,256,16,128]{3,1,0,2:T(8,128)(2,1)} %bitcast.56), calls=%async_computation.3 | async-start | bytes 4194304 | tf_op jit(solution)/shard_map/all_to_all | solution.py:75
  97.5 0.1 reshape.62
  97.6 2.7 %bitcast_convert_fusion = f32[256,128,16]{1,0,2:T(8,128)} fusion(bf16[16,256,2048]{2,1,0:T(8,128)(2,1)} %param.14, s32[]{:T(128)S(6)} %select_n.12), kind=kLoop, calls=%fused_computation.12 | loop fusion | flops 524288 | bytes 3145732
  100.4 26.1 %all-to-all-done.3 = bf16[2,256,16,128]{3,1,0,2:T(8,128)(2,1)S(1)} async-done(((bf16[2,256,16,128]{3,1,0,2:T(8,128)(2,1)}), bf16[2,256,16,128]{3,1,0,2:T(8,128)(2,1)S(1)}, u32[]{:S(2)}, u32[]{:S(2)}) %all-to-all-start.3) | async-done | bytes 2097184 | tf_op jit(solution)/shard_map/all_to_all | solution.py:75
  126.4 0.6 broadcast_in_dim.24
  127.1 0.7 copy-done.1
  127.8 3.7 %all-to-all-start.1 = ((bf16[8,2,256]{2,1,0:T(2,128)(2,1)}), bf16[8,2,256]{2,1,0:T(2,128)(2,1)S(1)}, u32[]{:S(2)}, u32[]{:S(2)}) async-start(bf16[8,2,256]{2,1,0:T(2,128)(2,1)} %broadcast_in_dim.24), calls=%async_computation.1 | async-start | bytes 16384 | tf_op jit(solution)/shard_map/all_to_all | solution.py:10
  131.5 1.7 copy.34
  133.2 13.9 %gather_fusion = bf16[256,2,256,128]{3,2,1,0:T(8,128)(2,1)} fusion(bf16[2,256,16,128]{3,1,2,0:T(8,128)(2,1)S(1)} %copy.34, s32[1024]{0:T(1024)S(1)} %pad_clamp_fusion), kind=kCustom, calls=%fused_computation | custom fusion | bytes 67109888 | tf_op jit(solution)/shard_map/jit(_take)/gather | solution.py:74
  147.1 17.9 %multiply_reduce_fusion = bf16[256,128,2,16]{1,0,2,3:T(8,128)(2,1)S(1)} fusion(f32[256,128,16]{1,0,2:T(8,128)} %bitcast_convert_fusion, bf16[16,16,2,256,128]{4,3,2,1,0:T(8,128)(2,1)} %bitcast.55, pred[16,16]{1,0:T(8,128)(4,1)S(1)} %compare_and_fusion), kind=kLoop, calls=%fused_computation.1 | loop fusion | flops 66060288 | bytes 37748992
  165.0 2.6 %copy.47 = bf16[256,128,2,16]{0,1,2,3:T(8,128)(2,1)} copy(bf16[256,128,2,16]{1,0,2,3:T(8,128)(2,1)S(1)} %multiply_reduce_fusion) | data formatting | bytes 4194304 | tf_op jit(solution)/shard_map/vrkqc,qrc->vrkc/dot_general | solution.py:79
  167.6 6.0 %all-to-all-start.4 = ((bf16[2,256,16,128]{1,3,0,2:T(8,128)(2,1)}), bf16[2,256,16,128]{1,3,0,2:T(8,128)(2,1)S(1)}, u32[]{:S(2)}, u32[]{:S(2)}) async-start(bf16[2,256,16,128]{1,3,0,2:T(8,128)(2,1)} %bitcast.57), calls=%async_computation.4 | async-start | bytes 4194304 | tf_op jit(solution)/shard_map/all_to_all | solution.py:82
  173.6 0.4 convolution_multiply_fusion
  174.0 28.5 %all-to-all-done.4 = bf16[2,256,16,128]{1,3,0,2:T(8,128)(2,1)S(1)} async-done(((bf16[2,256,16,128]{1,3,0,2:T(8,128)(2,1)}), bf16[2,256,16,128]{1,3,0,2:T(8,128)(2,1)S(1)}, u32[]{:S(2)}, u32[]{:S(2)}) %all-to-all-start.4) | async-done | bytes 2097184 | tf_op jit(solution)/shard_map/all_to_all | solution.py:82
  202.5 1.5 copy.35
  204.0 5.6 %fusion.2 = f32[2,896,128]{2,1,0:T(8,128)S(1)} fusion(bf16[2,256,2048]{1,2,0:T(8,128)(2,1)} %bitcast.58, bf16[2048,896,1]{1,0,2:T(8,128)(2,1)} %bitcast.12, f32[2,256]{1,0:T(2,128)S(1)} %convolution_multiply_fusion, f32[256,896]{0,1:T(8,128)} %copy-done.2, bf16[1,256,128]{2,1,0:T(8,128)(2,1)S(1)} %copy-done.5), kind=kOutput, calls=%fused_computation.10 | convolution fusion | flops 1997864960 | bytes 7669760 | tf_op jit(solution)/shard_map/ri,vra->via/dot_general | solution.py:90
  209.6 1.0 copy.56
  210.6 6.6 %all-to-all-start.5 = ((f32[8,2,128,112]{2,3,1,0:T(8,128)}), f32[8,2,128,112]{2,3,1,0:T(8,128)S(1)}, u32[]{:S(2)}, u32[]{:S(2)}) async-start(f32[8,2,128,112]{2,3,1,0:T(8,128)} %bitcast.54), calls=%async_computation.5 | async-start | bytes 1835008 | tf_op jit(solution)/shard_map/all_to_all | solution.py:35
  217.2 0.1 broadcast_subtract_fusion
  217.3 13.9 %all-to-all-done.5 = f32[8,2,128,112]{2,3,1,0:T(8,128)S(1)} async-done(((f32[8,2,128,112]{2,3,1,0:T(8,128)}), f32[8,2,128,112]{2,3,1,0:T(8,128)S(1)}, u32[]{:S(2)}, u32[]{:S(2)}) %all-to-all-start.5) | async-done | bytes 917536 | tf_op jit(solution)/shard_map/all_to_all | solution.py:35
  231.2 0.7 bitcast_add_fusion
  (25 shorter events, 0.2 us)
Async XLA Ops:
  0.0 173.6 %copy-start = (bf16[256,2048]{1,0:T(8,128)(2,1)S(1)}, bf16[256,2048]{1,0:T(8,128)(2,1)}, u32[]{:S(2)}) copy-start(bf16[256,2048]{1,0:T(8,128)(2,1)} %param.13) | copy-start | bytes 3145732
  3.4 5.5 %copy-start.3 = (bf16[1,256,896]{2,1,0:T(8,128)(2,1)S(1)}, bf16[1,256,896]{2,1,0:T(8,128)(2,1)}, u32[]{:S(2)}) copy-start(bf16[1,256,896]{2,1,0:T(8,128)(2,1)} %param.9) | copy-start | bytes 1376260
  3.4 73.1 %all-to-all-start.2 = ((bf16[8,256,896]{2,1,0:T(8,128)(2,1)}), bf16[8,256,896]{2,1,0:T(8,128)(2,1)}, u32[]{:S(2)}, u32[]{:S(2)}) async-start(bf16[8,256,896]{2,1,0:T(8,128)(2,1)} %stack.3), calls=%async_computation.2 | async-start | bytes 7340032 | tf_op jit(solution)/shard_map/all_to_all | solution.py:49
  8.9 0.9 copy-start.4
  8.9 67.1 %copy-start.5 = (bf16[1,256,128]{2,1,0:T(8,128)(2,1)S(1)}, bf16[1,256,128]{2,1,0:T(8,128)(2,1)}, u32[]{:S(2)}) copy-start(bf16[1,256,128]{2,1,0:T(8,128)(2,1)} %param.8) | copy-start | bytes 196612
  9.8 78.4 %copy-start.2 = (f32[256,896]{0,1:T(8,128)}, f32[256,896]{0,1:T(8,128)S(1)}, u32[]{:S(2)}) copy-start(f32[256,896]{0,1:T(8,128)S(1)} %copy.30) | copy-start | bytes 2752516
  77.1 13.0 %all-to-all-start = ((f32[16,2,256]{2,1,0:T(2,128)}), f32[16,2,256]{2,1,0:T(2,128)S(1)}, u32[]{:S(2)}, u32[]{:S(2)}) async-start(f32[16,2,256]{2,1,0:T(2,128)} %broadcast_in_dim.23), calls=%async_computation | async-start | bytes 65536 | tf_op jit(solution)/shard_map/all_to_all | solution.py:10
  90.2 7.4 %copy-start.6 = (s32[16,16]{1,0:T(8,128)S(1)}, s32[16,16]{1,0:T(8,128)}, u32[]{:S(2)}) copy-start(s32[16,16]{1,0:T(8,128)} %param.15) | copy-start | bytes 3076
  90.2 36.3 %all-to-all-start.3 = ((bf16[2,256,16,128]{3,1,0,2:T(8,128)(2,1)}), bf16[2,256,16,128]{3,1,0,2:T(8,128)(2,1)S(1)}, u32[]{:S(2)}, u32[]{:S(2)}) async-start(bf16[2,256,16,128]{3,1,0,2:T(8,128)(2,1)} %bitcast.56), calls=%async_computation.3 | async-start | bytes 4194304 | tf_op jit(solution)/shard_map/all_to_all | solution.py:75
  126.4 1.3 copy-start.1
  127.8 39.9 %all-to-all-start.1 = ((bf16[8,2,256]{2,1,0:T(2,128)(2,1)}), bf16[8,2,256]{2,1,0:T(2,128)(2,1)S(1)}, u32[]{:S(2)}, u32[]{:S(2)}) async-start(bf16[8,2,256]{2,1,0:T(2,128)(2,1)} %broadcast_in_dim.24), calls=%async_computation.1 | async-start | bytes 16384 | tf_op jit(solution)/shard_map/all_to_all | solution.py:10
  167.6 34.9 %all-to-all-start.4 = ((bf16[2,256,16,128]{1,3,0,2:T(8,128)(2,1)}), bf16[2,256,16,128]{1,3,0,2:T(8,128)(2,1)S(1)}, u32[]{:S(2)}, u32[]{:S(2)}) async-start(bf16[2,256,16,128]{1,3,0,2:T(8,128)(2,1)} %bitcast.57), calls=%async_computation.4 | async-start | bytes 4194304 | tf_op jit(solution)/shard_map/all_to_all | solution.py:82
  209.6 7.6 %copy-start.7 = (f32[1,128]{1,0:T(1,128)S(1)}, f32[1,128]{1,0:T(1,128)}, u32[]{:S(2)}) copy-start(f32[1,128]{1,0:T(1,128)} %param.11) | copy-start | bytes 1540
  209.6 7.6 %copy-start.8 = (f32[1,112]{1,0:T(1,128)S(1)}, f32[1,112]{1,0:T(1,128)}, u32[]{:S(2)}) copy-start(f32[1,112]{1,0:T(1,128)} %param.12) | copy-start | bytes 1348
  210.6 20.6 %all-to-all-start.5 = ((f32[8,2,128,112]{2,3,1,0:T(8,128)}), f32[8,2,128,112]{2,3,1,0:T(8,128)S(1)}, u32[]{:S(2)}, u32[]{:S(2)}) async-start(f32[8,2,128,112]{2,3,1,0:T(8,128)} %bitcast.54), calls=%async_computation.5 | async-start | bytes 1835008 | tf_op jit(solution)/shard_map/all_to_all | solution.py:35
